TPU v7x, 32 devices: a whole 2x2x4 slice. The times are simulated.
32 devices in a mesh: dom: 32 (over z, y, x, core).
Axes of the slice: x: 2, y: 2, z: 4, core: 2. Of those that a mesh axis runs over, the one named last changes fastest.
Arguments:
- node_emb: bfloat16 [16384, 64], P('dom'), may hold values from -6 to 6
- hub_emb: bfloat16 [256, 64], replicated, may hold values from -6 to 6
- tile_vals: bfloat16 [4096, 128, 128], P('dom')
- tile_col: int32 [4096], P('dom'), may hold values from 0 to 5
- tile_dest: int32 [4096], P('dom'), may hold values from 0 to 29, as said below
Outputs:
- node_out: float32 [16384, 64], P('dom')
- hub_out: float32 [256, 64], replicated
Inputs may be any that keep to these rules, and one draw needn't show every extreme that they name: tile_dest below 28 names a partition offset from -3 to 3 and a block of that partition; from 28 up it names a hub block. tile_col below 4 names one of the holding partition's own blocks; from 4 up it names a hub block.
All inputs are finite; a program needn't handle non-finite values.
Results may differ from a plain program's by a relative error of at most 0.0003.
Values sent between devices are 32-bit elements.
A program may use at most 64 MiB of HBM per device.

v0:
```python
import jax
import jax.numpy as jnp
from jax import lax
from jax.sharding import PartitionSpec as P

REACH_BITS = 2
LAYERS = 2


def shifted(block, axis, distance):
    devices = range(lax.axis_size(axis))
    route = [((i - distance) % len(devices), i) for i in devices]
    return lax.ppermute(block, axis, route)


def route_partials(spread, farthest):
    overall = spread[farthest]
    for heading in (1, -1):
        for distance in range(1, farthest + 1):
            overall = overall + shifted(
                spread[farthest + heading * distance], "dom", heading * distance
            )
    return overall


def shards(node_emb, hub_emb, tile_vals, tile_col, tile_dest):
    tile_size = tile_vals.shape[1]
    features = node_emb.shape[1]
    dev_rows = node_emb.shape[0]
    own_blocks = dev_rows // tile_size
    hub_rows = hub_emb.shape[0]
    hub_blocks = hub_rows // tile_size
    tile_count = tile_vals.shape[0]
    farthest = 2**REACH_BITS - 1
    slot_count = 2 * farthest + 1
    target_count = slot_count * own_blocks + hub_blocks
    one_hot = (tile_dest[None, :] == jnp.arange(target_count, dtype=jnp.int32)[:, None]).astype(
        jnp.float32
    )
    current_node = node_emb
    current_hub = hub_emb
    node_total = node_emb.astype(jnp.float32)
    hub_total = hub_emb.astype(jnp.float32)
    for layer_index in range(LAYERS):
        sources = jnp.concatenate([current_node, current_hub], 0).reshape(
            own_blocks + hub_blocks, tile_size, features
        )
        picked = jnp.take(sources, tile_col, axis=0)
        products = jnp.einsum("tij,tjd->tid", tile_vals, picked, preferred_element_type=jnp.float32)
        summed = jnp.dot(
            one_hot,
            products.reshape(tile_count, tile_size * features),
            precision=lax.Precision.HIGHEST,
            preferred_element_type=jnp.float32,
        )
        spread = summed[: slot_count * own_blocks].reshape(slot_count, dev_rows, features)
        hub_part = summed[slot_count * own_blocks :].reshape(hub_rows, features)
        hub_sum = lax.psum(hub_part, "dom")
        node_sum = route_partials(spread, farthest)
        node_total = node_total + node_sum
        hub_total = hub_total + hub_sum
        current_node = node_sum.astype(jnp.bfloat16)
        current_hub = hub_sum.astype(jnp.bfloat16)
    return (node_total / float(LAYERS + 1), hub_total / float(LAYERS + 1))


def solution(mesh):
    in_specs = (P("dom", None), P(), P("dom", None, None), P("dom"), P("dom"))
    out_specs = (P("dom", None), P())
    return jax.shard_map(shards, mesh=mesh, in_specs=in_specs, out_specs=out_specs, check_vma=False)
```

profile of v0, /device:TPU:0, one launch (start us, length us, event | category | flops | bytes accessed | tf_op | source)
XLA Modules:
  0.0 331.4 jit_solution(637796549837110401)
XLA Ops:
  8.5 0.9 copy_bitcast_fusion
  9.4 1.0 gather_fusion
  10.4 7.1 %convolution_bitcast_fusion.1 = f32[128,128,64]{1,2,0:T(8,128)} fusion(bf16[128,128,128]{2,1,0:T(8,128)(2,1)} %param.9, bf16[128,128,64]{1,2,0:T(8,128)(2,1)S(1)} %gather_fusion, pred[128]{0:T(512)(128)(4,1)S(1)} %compare_and_fusion), kind=kOutput, calls=%fused_computation.3 | convolution fusion | flops 269484032 | bytes 10485888 | tf_op jit(solution)/shard_map/tij,tjd->tid/dot_general | solution.py:49
  17.5 5.5 %copy.25 = f32[128,128,64]{0,2,1:T(8,128)} copy(f32[128,128,64]{1,2,0:T(8,128)} %convolution_bitcast_fusion.1) | data formatting | bytes 8388608 | tf_op jit(solution)/shard_map/tij,tjd->tid/dot_general | solution.py:49
  22.9 4.6 %fusion.7 = f32[30,8192]{1,0:T(8,128)S(1)} fusion(f32[128,8192]{0,1:T(8,128)} %bitcast.16, s32[128]{0:T(128)S(1)} %copy-done.3), kind=kOutput, calls=%fused_computation.18 | convolution fusion | flops 377491200 | bytes 5177856 | tf_op jit(solution)/shard_map/dot_general | solution.py:50
  28.5 2.5 collective-permute-start.1
  31.3 2.4 collective-permute-start.2
  33.7 0.9 squeeze.46
  34.6 3.0 collective-permute-start.3
  38.4 1.2 collective-permute-start.4
  40.5 2.4 collective-permute-done
  44.1 124.6 %all-reduce.3.cloned.1.call-done = f32[256,64]{1,0:T(8,128)} async-done(((f32[256,64]{1,0:T(8,128)}), f32[256,64]{1,0:T(8,128)}) %all-reduce.3.cloned.1.call-update) | async-done | bytes 65552 | tf_op jit(solution)/shard_map/psum | solution.py:58
  168.7 0.9 convert_element_type.15
  169.9 1.0 gather_fusion.1
  170.9 7.1 %convolution_bitcast_fusion = f32[128,128,64]{1,2,0:T(8,128)} fusion(bf16[128,128,128]{2,1,0:T(8,128)(2,1)} %param.9, bf16[128,128,64]{1,2,0:T(8,128)(2,1)S(1)} %gather_fusion.1, pred[128]{0:T(512)(128)(4,1)S(1)} %compare_and_fusion), kind=kOutput, calls=%fused_computation.2 | convolution fusion | flops 269484032 | bytes 10485888 | tf_op jit(solution)/shard_map/tij,tjd->tid/dot_general | solution.py:49
  178.0 5.4 %copy.28 = f32[128,128,64]{0,2,1:T(8,128)} copy(f32[128,128,64]{1,2,0:T(8,128)} %convolution_bitcast_fusion) | data formatting | bytes 8388608 | tf_op jit(solution)/shard_map/tij,tjd->tid/dot_general | solution.py:49
  183.4 4.6 %fusion.6 = f32[30,8192]{1,0:T(8,128)S(1)} fusion(f32[128,8192]{0,1:T(8,128)} %bitcast.17, s32[128]{0:T(128)S(1)} %copy-done.3), kind=kOutput, calls=%fused_computation.17 | convolution fusion | flops 377491200 | bytes 5177856 | tf_op jit(solution)/shard_map/dot_general | solution.py:50
  188.4 3.3 collective-permute-start.10
  193.0 0.9 squeeze.50
  193.9 1.6 collective-permute-start.6
  195.5 0.9 squeeze.51
  199.7 3.6 %collective-permute-start.9 = (f32[512,64]{1,0:T(8,128)}, f32[512,64]{1,0:T(8,128)S(1)}, u32[]{:S(2)}, u32[]{:S(2)}) collective-permute-start(f32[512,64]{1,0:T(8,128)} %squeeze.53), channel_id=1, source_target_pairs={{1,0},{2,1},{3,2},{4,3},{5,4},{6,5},{7,6},{8,7},{9,8},{10,9},{11,1... | collective-permute-start | bytes 393224 | tf_op jit(solution)/shard_map/ppermute | solution.py:13
  203.3 118.6 %all-reduce.5.cloned.1.call-done = f32[256,64]{1,0:T(8,128)} async-done(((f32[256,64]{1,0:T(8,128)}), f32[256,64]{1,0:T(8,128)}) %all-reduce.5.cloned.1.call-update) | async-done | bytes 65552 | tf_op jit(solution)/shard_map/psum | solution.py:58
  321.9 0.9 add_multiply_fusion.1
  (56 shorter events, 12.4 us)
Async XLA Ops:
  7.2 161.5 %all-reduce.3.cloned.1.call-start = ((), (), s32[]{:S(2)}) async-start(), calls=%async_computation | async-start | bytes 262144 | tf_op jit(solution)/shard_map/psum | solution.py:58
  17.5 5.5 %copy-start.3 = (s32[128]{0:T(128)S(1)}, s32[128]{0:T(128)}, u32[]{:S(2)}) copy-start(s32[128]{0:T(128)} %param.11) | copy-start | bytes 1540
  27.8 15.0 %collective-permute-start = (f32[512,64]{1,0:T(8,128)S(1)}, f32[512,64]{1,0:T(8,128)S(1)}, u32[]{:S(2)}, u32[]{:S(2)}) collective-permute-start(f32[512,64]{1,0:T(8,128)S(1)} %squeeze.43), channel_id=1, source_target_pairs={{31,0},{0,1},{1,2},{2,3},{3,4},{4,5},{5,6},{6,7},{7,8},{8,9},{9,10... | collective-permute-start | bytes 393224 | tf_op jit(solution)/shard_map/ppermute | solution.py:13
  28.5 141.1 %collective-permute-start.1 = (f32[512,64]{1,0:T(8,128)S(1)}, f32[512,64]{1,0:T(8,128)S(1)}, u32[]{:S(2)}, u32[]{:S(2)}) collective-permute-start(f32[512,64]{1,0:T(8,128)S(1)} %squeeze.44), channel_id=1, source_target_pairs={{30,0},{31,1},{0,2},{1,3},{2,4},{3,5},{4,6},{5,7},{6,8},{7,9},{8,1... | collective-permute-start | bytes 393224 | tf_op jit(solution)/shard_map/ppermute | solution.py:13
  31.3 138.4 %collective-permute-start.2 = (f32[512,64]{1,0:T(8,128)S(1)}, f32[512,64]{1,0:T(8,128)S(1)}, u32[]{:S(2)}, u32[]{:S(2)}) collective-permute-start(f32[512,64]{1,0:T(8,128)S(1)} %squeeze.45), channel_id=1, source_target_pairs={{29,0},{30,1},{31,2},{0,3},{1,4},{2,5},{3,6},{4,7},{5,8},{6,9},{7,... | collective-permute-start | bytes 393224 | tf_op jit(solution)/shard_map/ppermute | solution.py:13
  34.6 135.0 %collective-permute-start.3 = (f32[512,64]{1,0:T(8,128)}, f32[512,64]{1,0:T(8,128)S(1)}, u32[]{:S(2)}, u32[]{:S(2)}) collective-permute-start(f32[512,64]{1,0:T(8,128)} %squeeze.46), channel_id=1, source_target_pairs={{1,0},{2,1},{3,2},{4,3},{5,4},{6,5},{7,6},{8,7},{9,8},{10,9},{11,1... | collective-permute-start | bytes 393224 | tf_op jit(solution)/shard_map/ppermute | solution.py:13
  38.4 131.2 %collective-permute-start.4 = (f32[512,64]{1,0:T(8,128)}, f32[512,64]{1,0:T(8,128)S(1)}, u32[]{:S(2)}, u32[]{:S(2)}) collective-permute-start(f32[512,64]{1,0:T(8,128)} %squeeze.47), channel_id=1, source_target_pairs={{2,0},{3,1},{4,2},{5,3},{6,4},{7,5},{8,6},{9,7},{10,8},{11,9},{12,... | collective-permute-start | bytes 393224 | tf_op jit(solution)/shard_map/ppermute | solution.py:13
  42.9 126.8 %collective-permute-start.5 = (f32[512,64]{1,0:T(8,128)}, f32[512,64]{1,0:T(8,128)S(1)}, u32[]{:S(2)}, u32[]{:S(2)}) collective-permute-start(f32[512,64]{1,0:T(8,128)} %squeeze.48), channel_id=1, source_target_pairs={{3,0},{4,1},{5,2},{6,3},{7,4},{8,5},{9,6},{10,7},{11,8},{12,9},{13... | collective-permute-start | bytes 393224 | tf_op jit(solution)/shard_map/ppermute | solution.py:13
  43.7 278.2 %all-reduce.5.cloned.1.call-start = ((), (), s32[]{:S(2)}) async-start(), calls=%async_computation.1 | async-start | bytes 262144 | tf_op jit(solution)/shard_map/psum | solution.py:58
  183.4 9.1 %copy-start.1 = (bf16[512,64]{0,1:T(8,128)(2,1)S(1)}, bf16[512,64]{0,1:T(8,128)(2,1)}, u32[]{:S(2)}) copy-start(bf16[512,64]{0,1:T(8,128)(2,1)} %param.7) | copy-start | bytes 196612
  183.4 9.2 %copy-start.2 = (bf16[256,64]{0,1:T(8,128)(2,1)S(1)}, bf16[256,64]{0,1:T(8,128)(2,1)}, u32[]{:S(2)}) copy-start(bf16[256,64]{0,1:T(8,128)(2,1)} %param.8) | copy-start | bytes 98308
  183.4 138.5 %copy-start = (f32[256,64]{1,0:T(8,128)S(1)}, f32[256,64]{1,0:T(8,128)}, u32[]{:S(2)}) copy-start(f32[256,64]{1,0:T(8,128)} %all-reduce.3.cloned.1.call-done) | copy-start | bytes 196612
  188.4 11.3 %collective-permute-start.10 = (f32[512,64]{1,0:T(8,128)S(1)}, f32[512,64]{1,0:T(8,128)S(1)}, u32[]{:S(2)}, u32[]{:S(2)}) collective-permute-start(f32[512,64]{1,0:T(8,128)S(1)} %squeeze.54), channel_id=1, source_target_pairs={{2,0},{3,1},{4,2},{5,3},{6,4},{7,5},{8,6},{9,7},{10,8},{11,9},{12,... | collective-permute-start | bytes 393224 | tf_op jit(solution)/shard_map/ppermute | solution.py:13
  193.0 130.6 %collective-permute-start.11 = (f32[512,64]{1,0:T(8,128)S(1)}, f32[512,64]{1,0:T(8,128)S(1)}, u32[]{:S(2)}, u32[]{:S(2)}) collective-permute-start(f32[512,64]{1,0:T(8,128)S(1)} %squeeze.55), channel_id=1, source_target_pairs={{3,0},{4,1},{5,2},{6,3},{7,4},{8,5},{9,6},{10,7},{11,8},{12,9},{13... | collective-permute-start | bytes 393224 | tf_op jit(solution)/shard_map/ppermute | solution.py:13
  193.9 129.7 %collective-permute-start.6 = (f32[512,64]{1,0:T(8,128)}, f32[512,64]{1,0:T(8,128)S(1)}, u32[]{:S(2)}, u32[]{:S(2)}) collective-permute-start(f32[512,64]{1,0:T(8,128)} %squeeze.50), channel_id=1, source_target_pairs={{31,0},{0,1},{1,2},{2,3},{3,4},{4,5},{5,6},{6,7},{7,8},{8,9},{9,10... | collective-permute-start | bytes 393224 | tf_op jit(solution)/shard_map/ppermute | solution.py:13
  196.4 127.2 %collective-permute-start.7 = (f32[512,64]{1,0:T(8,128)}, f32[512,64]{1,0:T(8,128)S(1)}, u32[]{:S(2)}, u32[]{:S(2)}) collective-permute-start(f32[512,64]{1,0:T(8,128)} %squeeze.51), channel_id=1, source_target_pairs={{30,0},{31,1},{0,2},{1,3},{2,4},{3,5},{4,6},{5,7},{6,8},{7,9},{8,1... | collective-permute-start | bytes 393224 | tf_op jit(solution)/shard_map/ppermute | solution.py:13
  197.8 125.8 %collective-permute-start.8 = (f32[512,64]{1,0:T(8,128)}, f32[512,64]{1,0:T(8,128)S(1)}, u32[]{:S(2)}, u32[]{:S(2)}) collective-permute-start(f32[512,64]{1,0:T(8,128)} %squeeze.52), channel_id=1, source_target_pairs={{29,0},{30,1},{31,2},{0,3},{1,4},{2,5},{3,6},{4,7},{5,8},{6,9},{7,... | collective-permute-start | bytes 393224 | tf_op jit(solution)/shard_map/ppermute | solution.py:13
  199.7 123.9 %collective-permute-start.9 = (f32[512,64]{1,0:T(8,128)}, f32[512,64]{1,0:T(8,128)S(1)}, u32[]{:S(2)}, u32[]{:S(2)}) collective-permute-start(f32[512,64]{1,0:T(8,128)} %squeeze.53), channel_id=1, source_target_pairs={{1,0},{2,1},{3,2},{4,3},{5,4},{6,5},{7,6},{8,7},{9,8},{10,9},{11,1... | collective-permute-start | bytes 393224 | tf_op jit(solution)/shard_map/ppermute | solution.py:13
Sparse Core Ops, SparseCore 0:
  43.8 124.8 all-reduce.2
  192.7 129.2 all-reduce.4
where the time goes:
time: 332 us; the launch traced here: 331 us
  waiting for transfers between devices  246 us (74%)
  local copies, waits for them, and re-layouts  24.1 us (7%)
  matrix products  23.3 us (7%)
  starting transfers between devices  19 us (6%)
  between operations  14.2 us (4%)
  other arithmetic  4.29 us (1%)
    psum x2, waiting for transfers between devices, shards(): hub_sum = lax.psum(hub_part, 'dom')  243 us
    ppermute x12, starting transfers between devices, shifted(): return lax.ppermute(block, axis, route)  18.7 us
    dot_general x2, matrix products, shards(): jnp.einsum('tij,tjd->tid', tile_vals, picked, preferred_element_type=jnp....  14.1 us
    dot_general x2, local copies, waits for them, and re-layouts, shards(): jnp.einsum('tij,tjd->tid', tile_vals, picked, preferred_element_type=jnp....  10.9 us
    dot_general x2, matrix products, shards(): jnp.dot(one_hot, products.reshape(tile_count, tile_size * features), prec...  9.19 us
    squeeze x12, local copies, waits for them, and re-layouts, route_partials(): spread[farthest + heading * distance]  7.08 us
  transfers between devices with their start and end apart: 14, of which 4 were waited for; matrix products, arithmetic and copies ran while one was open for 3% of the time, Pallas kernels for 0%

commit v1 on v0

--- a/solution.py
+++ b/solution.py
@@ -55,7 +55,7 @@
         )
         spread = summed[: slot_count * own_blocks].reshape(slot_count, dev_rows, features)
         hub_part = summed[slot_count * own_blocks :].reshape(hub_rows, features)
-        hub_sum = lax.psum(hub_part, "dom")
+        hub_sum = jnp.sum(lax.all_gather(hub_part, "dom"), axis=0)
         node_sum = route_partials(spread, farthest)
         node_total = node_total + node_sum
         hub_total = hub_total + hub_sum

time: 332 us -> 197 us (0.59)
  waiting for transfers between devices: 246 us -> 109 us
    psum x2 -> x0, waiting for transfers between devices: 243 us -> none  [shards(): hub_sum = lax.psum(hub_part, 'dom')]
    all_gather x0 -> x2, waiting for transfers between devices: none -> 80.9 us  [shards(): hub_sum = jnp.sum(lax.all_gather(hub_part, 'dom'), axis=0)]
    ppermute x12, waiting for transfers between devices: 3.24 us -> 28.4 us  [shifted(): return lax.ppermute(block, axis, route)]
    reduce_sum x0 -> x2, other arithmetic: none -> 3.43 us  [shards(): hub_sum = jnp.sum(lax.all_gather(hub_part, 'dom'), axis=0)]
  transfers between devices with their start and end apart: 14 -> 14, of which waited for: 4 -> 10; matrix products, arithmetic and copies ran while one was open for 3% -> 3% of each run, Pallas kernels for 0% -> 0%
where the time goes in v1:
time: 197 us; the launch traced here: 196 us
  waiting for transfers between devices  109 us (55%)
  matrix products  23.3 us (12%)
  local copies, waits for them, and re-layouts  21.5 us (11%)
  starting transfers between devices  21.1 us (11%)
  between operations  14.2 us (7%)
  other arithmetic  6.53 us (3%)
    all_gather x2, waiting for transfers between devices, shards(): hub_sum = jnp.sum(lax.all_gather(hub_part, 'dom'), axis=0)  80.9 us
    ppermute x12, waiting for transfers between devices, shifted(): return lax.ppermute(block, axis, route)  28.4 us
    ppermute x12, starting transfers between devices, shifted(): return lax.ppermute(block, axis, route)  21.1 us
    dot_general x2, matrix products, shards(): jnp.einsum('tij,tjd->tid', tile_vals, picked, preferred_element_type=jnp....  14.2 us
    dot_general x2, local copies, waits for them, and re-layouts, shards(): jnp.einsum('tij,tjd->tid', tile_vals, picked, preferred_element_type=jnp....  11 us
    dot_general x2, matrix products, shards(): jnp.dot(one_hot, products.reshape(tile_count, tile_size * features), prec...  9.19 us
    squeeze x12, local copies, waits for them, and re-layouts, route_partials(): spread[farthest + heading * distance]  5.07 us
  transfers between devices with their start and end apart: 14, of which 10 were waited for; matrix products, arithmetic and copies ran while one was open for 3% of the time, Pallas kernels for 0%

profile of v1, /device:TPU:0, one launch (start us, length us, event | category | flops | bytes accessed | tf_op | source)
XLA Modules:
  0.0 196.1 jit_solution(5008848456689445085)
XLA Ops:
  10.4 7.1 %convolution_bitcast_fusion.1 = f32[128,128,64]{1,2,0:T(8,128)} fusion(bf16[128,128,128]{2,1,0:T(8,128)(2,1)} %param.9, bf16[128,128,64]{1,2,0:T(8,128)(2,1)S(1)} %gather_fusion, pred[128]{0:T(512)(128)(4,1)S(1)} %compare_and_fusion), kind=kOutput, calls=%fused_computation.3 | convolution fusion | flops 269484032 | bytes 10485888 | tf_op jit(solution)/shard_map/tij,tjd->tid/dot_general | solution.py:49
  17.5 5.5 %copy.43 = f32[128,128,64]{0,2,1:T(8,128)} copy(f32[128,128,64]{1,2,0:T(8,128)} %convolution_bitcast_fusion.1) | data formatting | bytes 8388608 | tf_op jit(solution)/shard_map/tij,tjd->tid/dot_general | solution.py:49
  23.0 4.6 %fusion.7 = f32[30,8192]{1,0:T(8,128)S(1)} fusion(f32[128,8192]{0,1:T(8,128)} %bitcast.16, s32[128]{0:T(128)S(1)} %copy-done.2), kind=kOutput, calls=%fused_computation.18 | convolution fusion | flops 377491200 | bytes 5177856 | tf_op jit(solution)/shard_map/dot_general | solution.py:50
  29.5 2.5 %collective-permute-start.1 = (f32[512,64]{1,0:T(8,128)S(1)}, f32[512,64]{1,0:T(8,128)S(1)}, u32[]{:S(2)}, u32[]{:S(2)}) collective-permute-start(f32[512,64]{1,0:T(8,128)S(1)} %squeeze.44), channel_id=1, source_target_pairs={{30,0},{31,1},{0,2},{1,3},{2,4},{3,5},{4,6},{5,7},{6,8},{7,9},{8,1... | collective-permute-start | bytes 393224 | tf_op jit(solution)/shard_map/ppermute | solution.py:13
  32.3 2.4 %collective-permute-start.2 = (f32[512,64]{1,0:T(8,128)S(1)}, f32[512,64]{1,0:T(8,128)S(1)}, u32[]{:S(2)}, u32[]{:S(2)}) collective-permute-start(f32[512,64]{1,0:T(8,128)S(1)} %squeeze.45), channel_id=1, source_target_pairs={{29,0},{30,1},{31,2},{0,3},{1,4},{2,5},{3,6},{4,7},{5,8},{6,9},{7,... | collective-permute-start | bytes 393224 | tf_op jit(solution)/shard_map/ppermute | solution.py:13
  34.9 3.0 %collective-permute-start.3 = (f32[512,64]{1,0:T(8,128)S(1)}, f32[512,64]{1,0:T(8,128)S(1)}, u32[]{:S(2)}, u32[]{:S(2)}) collective-permute-start(f32[512,64]{1,0:T(8,128)S(1)} %squeeze.46), channel_id=1, source_target_pairs={{1,0},{2,1},{3,2},{4,3},{5,4},{6,5},{7,6},{8,7},{9,8},{10,9},{11,1... | collective-permute-start | bytes 393224 | tf_op jit(solution)/shard_map/ppermute | solution.py:13
  38.1 1.2 collective-permute-start.4
  40.2 3.8 %collective-permute-done = f32[512,64]{1,0:T(8,128)S(1)} collective-permute-done((f32[512,64]{1,0:T(8,128)S(1)}, f32[512,64]{1,0:T(8,128)S(1)}, u32[]{:S(2)}, u32[]{:S(2)}) %collective-permute-start) | collective-permute-done | bytes 131104 | tf_op jit(solution)/shard_map/ppermute | solution.py:13
  44.1 2.0 %collective-permute-done.1 = f32[512,64]{1,0:T(8,128)S(1)} collective-permute-done((f32[512,64]{1,0:T(8,128)S(1)}, f32[512,64]{1,0:T(8,128)S(1)}, u32[]{:S(2)}, u32[]{:S(2)}) %collective-permute-start.1) | collective-permute-done | bytes 131104 | tf_op jit(solution)/shard_map/ppermute | solution.py:13
  46.1 9.2 %collective-permute-done.2 = f32[512,64]{1,0:T(8,128)S(1)} collective-permute-done((f32[512,64]{1,0:T(8,128)S(1)}, f32[512,64]{1,0:T(8,128)S(1)}, u32[]{:S(2)}, u32[]{:S(2)}) %collective-permute-start.2) | collective-permute-done | bytes 131104 | tf_op jit(solution)/shard_map/ppermute | solution.py:13
  55.3 2.0 %collective-permute-done.4 = f32[512,64]{1,0:T(8,128)S(1)} collective-permute-done((f32[512,64]{1,0:T(8,128)S(1)}, f32[512,64]{1,0:T(8,128)S(1)}, u32[]{:S(2)}, u32[]{:S(2)}) %collective-permute-start.4) | collective-permute-done | bytes 131104 | tf_op jit(solution)/shard_map/ppermute | solution.py:13
  57.4 41.3 %all-gather.3.cloned.1.call-done = f32[32,256,64]{1,2,0:T(8,128)} async-done(((f32[1,256,64]{1,2,0:T(8,128)}), f32[32,256,64]{1,2,0:T(8,128)}) %all-gather.3.cloned.1.call-update) | async-done | bytes 2097168 | tf_op jit(solution)/shard_map/all_gather | solution.py:58
  98.6 1.7 reduce_sum.18
  101.7 7.1 %convolution_bitcast_fusion = f32[128,128,64]{1,2,0:T(8,128)} fusion(bf16[128,128,128]{2,1,0:T(8,128)(2,1)} %param.9, bf16[128,128,64]{1,2,0:T(8,128)(2,1)S(1)} %gather_fusion.1, pred[128]{0:T(512)(128)(4,1)S(1)} %compare_and_fusion), kind=kOutput, calls=%fused_computation.2 | convolution fusion | flops 269484032 | bytes 10485888 | tf_op jit(solution)/shard_map/tij,tjd->tid/dot_general | solution.py:49
  108.7 5.5 %copy.48 = f32[128,128,64]{0,2,1:T(8,128)} copy(f32[128,128,64]{1,2,0:T(8,128)} %convolution_bitcast_fusion) | data formatting | bytes 8388608 | tf_op jit(solution)/shard_map/tij,tjd->tid/dot_general | solution.py:49
  114.2 4.6 %fusion.6 = f32[30,8192]{1,0:T(8,128)S(1)} fusion(f32[128,8192]{0,1:T(8,128)} %bitcast.17, s32[128]{0:T(128)S(1)} %copy-done.2), kind=kOutput, calls=%fused_computation.17 | convolution fusion | flops 377491200 | bytes 5177856 | tf_op jit(solution)/shard_map/dot_general | solution.py:50
  120.1 3.1 %collective-permute-start.10 = (f32[512,64]{1,0:T(8,128)S(1)}, f32[512,64]{1,0:T(8,128)S(1)}, u32[]{:S(2)}, u32[]{:S(2)}) collective-permute-start(f32[512,64]{1,0:T(8,128)S(1)} %squeeze.54), channel_id=1, source_target_pairs={{2,0},{3,1},{4,2},{5,3},{6,4},{7,5},{8,6},{9,7},{10,8},{11,9},{12,... | collective-permute-start | bytes 393224 | tf_op jit(solution)/shard_map/ppermute | solution.py:13
  123.4 1.0 collective-permute-start.11
  129.1 2.4 %collective-permute-done.10 = f32[512,64]{1,0:T(8,128)S(1)} collective-permute-done((f32[512,64]{1,0:T(8,128)S(1)}, f32[512,64]{1,0:T(8,128)S(1)}, u32[]{:S(2)}, u32[]{:S(2)}) %collective-permute-start.10) | collective-permute-done | bytes 131104 | tf_op jit(solution)/shard_map/ppermute | solution.py:13
  131.5 5.4 %collective-permute-start.9 = (f32[512,64]{1,0:T(8,128)}, f32[512,64]{1,0:T(8,128)S(1)}, u32[]{:S(2)}, u32[]{:S(2)}) collective-permute-start(f32[512,64]{1,0:T(8,128)} %squeeze.53), channel_id=1, source_target_pairs={{1,0},{2,1},{3,2},{4,3},{5,4},{6,5},{7,6},{8,7},{9,8},{10,9},{11,1... | collective-permute-start | bytes 393224 | tf_op jit(solution)/shard_map/ppermute | solution.py:13
  137.7 4.4 %collective-permute-done.7 = f32[512,64]{1,0:T(8,128)S(1)} collective-permute-done((f32[512,64]{1,0:T(8,128)}, f32[512,64]{1,0:T(8,128)S(1)}, u32[]{:S(2)}, u32[]{:S(2)}) %collective-permute-start.7) | collective-permute-done | bytes 131104 | tf_op jit(solution)/shard_map/ppermute | solution.py:13
  142.1 4.2 %collective-permute-done.8 = f32[512,64]{1,0:T(8,128)S(1)} collective-permute-done((f32[512,64]{1,0:T(8,128)}, f32[512,64]{1,0:T(8,128)S(1)}, u32[]{:S(2)}, u32[]{:S(2)}) %collective-permute-start.8) | collective-permute-done | bytes 131104 | tf_op jit(solution)/shard_map/ppermute | solution.py:13
  147.2 39.7 %all-gather.5.cloned.1.call-done = f32[32,256,64]{1,2,0:T(8,128)} async-done(((f32[1,256,64]{1,2,0:T(8,128)}), f32[32,256,64]{1,2,0:T(8,128)}) %all-gather.5.cloned.1.call-update) | async-done | bytes 2097168 | tf_op jit(solution)/shard_map/all_gather | solution.py:58
  186.8 1.7 reduce_sum.19
  (57 shorter events, 16.6 us)
Async XLA Ops:
  7.2 91.5 %all-gather.3.cloned.1.call-start = ((), (), s32[]{:S(2)}) async-start(), calls=%async_computation | async-start | bytes 2162688 | tf_op jit(solution)/shard_map/all_gather | solution.py:58
  17.5 5.5 %copy-start.2 = (s32[128]{0:T(128)S(1)}, s32[128]{0:T(128)}, u32[]{:S(2)}) copy-start(s32[128]{0:T(128)} %param.11) | copy-start | bytes 1540
  28.5 158.4 %all-gather.5.cloned.1.call-start = ((), (), s32[]{:S(2)}) async-start(), calls=%async_computation.1 | async-start | bytes 2162688 | tf_op jit(solution)/shard_map/all_gather | solution.py:58
  28.8 15.1 %collective-permute-start = (f32[512,64]{1,0:T(8,128)S(1)}, f32[512,64]{1,0:T(8,128)S(1)}, u32[]{:S(2)}, u32[]{:S(2)}) collective-permute-start(f32[512,64]{1,0:T(8,128)S(1)} %squeeze.43), channel_id=1, source_target_pairs={{31,0},{0,1},{1,2},{2,3},{3,4},{4,5},{5,6},{6,7},{7,8},{8,9},{9,10... | collective-permute-start | bytes 393224 | tf_op jit(solution)/shard_map/ppermute | solution.py:13
  29.5 16.6 %collective-permute-start.1 = (f32[512,64]{1,0:T(8,128)S(1)}, f32[512,64]{1,0:T(8,128)S(1)}, u32[]{:S(2)}, u32[]{:S(2)}) collective-permute-start(f32[512,64]{1,0:T(8,128)S(1)} %squeeze.44), channel_id=1, source_target_pairs={{30,0},{31,1},{0,2},{1,3},{2,4},{3,5},{4,6},{5,7},{6,8},{7,9},{8,1... | collective-permute-start | bytes 393224 | tf_op jit(solution)/shard_map/ppermute | solution.py:13
  32.3 23.0 %collective-permute-start.2 = (f32[512,64]{1,0:T(8,128)S(1)}, f32[512,64]{1,0:T(8,128)S(1)}, u32[]{:S(2)}, u32[]{:S(2)}) collective-permute-start(f32[512,64]{1,0:T(8,128)S(1)} %squeeze.45), channel_id=1, source_target_pairs={{29,0},{30,1},{31,2},{0,3},{1,4},{2,5},{3,6},{4,7},{5,8},{6,9},{7,... | collective-permute-start | bytes 393224 | tf_op jit(solution)/shard_map/ppermute | solution.py:13
  34.9 20.4 %collective-permute-start.3 = (f32[512,64]{1,0:T(8,128)S(1)}, f32[512,64]{1,0:T(8,128)S(1)}, u32[]{:S(2)}, u32[]{:S(2)}) collective-permute-start(f32[512,64]{1,0:T(8,128)S(1)} %squeeze.46), channel_id=1, source_target_pairs={{1,0},{2,1},{3,2},{4,3},{5,4},{6,5},{7,6},{8,7},{9,8},{10,9},{11,1... | collective-permute-start | bytes 393224 | tf_op jit(solution)/shard_map/ppermute | solution.py:13
  38.1 19.2 %collective-permute-start.4 = (f32[512,64]{1,0:T(8,128)S(1)}, f32[512,64]{1,0:T(8,128)S(1)}, u32[]{:S(2)}, u32[]{:S(2)}) collective-permute-start(f32[512,64]{1,0:T(8,128)S(1)} %squeeze.47), channel_id=1, source_target_pairs={{2,0},{3,1},{4,2},{5,3},{6,4},{7,5},{8,6},{9,7},{10,8},{11,9},{12,... | collective-permute-start | bytes 393224 | tf_op jit(solution)/shard_map/ppermute | solution.py:13
  44.0 13.3 %collective-permute-start.5 = (f32[512,64]{1,0:T(8,128)}, f32[512,64]{1,0:T(8,128)S(1)}, u32[]{:S(2)}, u32[]{:S(2)}) collective-permute-start(f32[512,64]{1,0:T(8,128)} %squeeze.48), channel_id=1, source_target_pairs={{3,0},{4,1},{5,2},{6,3},{7,4},{8,5},{9,6},{10,7},{11,8},{12,9},{13... | collective-permute-start | bytes 393224 | tf_op jit(solution)/shard_map/ppermute | solution.py:13
  114.2 22.7 %copy-start = (bf16[512,64]{0,1:T(8,128)(2,1)S(1)}, bf16[512,64]{0,1:T(8,128)(2,1)}, u32[]{:S(2)}) copy-start(bf16[512,64]{0,1:T(8,128)(2,1)} %param.7) | copy-start | bytes 196612
  119.9 68.7 %copy-start.1 = (bf16[256,64]{0,1:T(8,128)(2,1)S(1)}, bf16[256,64]{0,1:T(8,128)(2,1)}, u32[]{:S(2)}) copy-start(bf16[256,64]{0,1:T(8,128)(2,1)} %param.8) | copy-start | bytes 98308
  120.1 11.4 %collective-permute-start.10 = (f32[512,64]{1,0:T(8,128)S(1)}, f32[512,64]{1,0:T(8,128)S(1)}, u32[]{:S(2)}, u32[]{:S(2)}) collective-permute-start(f32[512,64]{1,0:T(8,128)S(1)} %squeeze.54), channel_id=1, source_target_pairs={{2,0},{3,1},{4,2},{5,3},{6,4},{7,5},{8,6},{9,7},{10,8},{11,9},{12,... | collective-permute-start | bytes 393224 | tf_op jit(solution)/shard_map/ppermute | solution.py:13
  123.4 14.3 %collective-permute-start.11 = (f32[512,64]{1,0:T(8,128)S(1)}, f32[512,64]{1,0:T(8,128)S(1)}, u32[]{:S(2)}, u32[]{:S(2)}) collective-permute-start(f32[512,64]{1,0:T(8,128)S(1)} %squeeze.55), channel_id=1, source_target_pairs={{3,0},{4,1},{5,2},{6,3},{7,4},{8,5},{9,6},{10,7},{11,8},{12,9},{13... | collective-permute-start | bytes 393224 | tf_op jit(solution)/shard_map/ppermute | solution.py:13
  124.6 13.1 %collective-permute-start.6 = (f32[512,64]{1,0:T(8,128)S(1)}, f32[512,64]{1,0:T(8,128)S(1)}, u32[]{:S(2)}, u32[]{:S(2)}) collective-permute-start(f32[512,64]{1,0:T(8,128)S(1)} %squeeze.50), channel_id=1, source_target_pairs={{31,0},{0,1},{1,2},{2,3},{3,4},{4,5},{5,6},{6,7},{7,8},{8,9},{9,10... | collective-permute-start | bytes 393224 | tf_op jit(solution)/shard_map/ppermute | solution.py:13
  126.1 16.0 %collective-permute-start.7 = (f32[512,64]{1,0:T(8,128)}, f32[512,64]{1,0:T(8,128)S(1)}, u32[]{:S(2)}, u32[]{:S(2)}) collective-permute-start(f32[512,64]{1,0:T(8,128)} %squeeze.51), channel_id=1, source_target_pairs={{30,0},{31,1},{0,2},{1,3},{2,4},{3,5},{4,6},{5,7},{6,8},{7,9},{8,1... | collective-permute-start | bytes 393224 | tf_op jit(solution)/shard_map/ppermute | solution.py:13
  127.6 18.7 %collective-permute-start.8 = (f32[512,64]{1,0:T(8,128)}, f32[512,64]{1,0:T(8,128)S(1)}, u32[]{:S(2)}, u32[]{:S(2)}) collective-permute-start(f32[512,64]{1,0:T(8,128)} %squeeze.52), channel_id=1, source_target_pairs={{29,0},{30,1},{31,2},{0,3},{1,4},{2,5},{3,6},{4,7},{5,8},{6,9},{7,... | collective-permute-start | bytes 393224 | tf_op jit(solution)/shard_map/ppermute | solution.py:13
  131.5 14.8 %collective-permute-start.9 = (f32[512,64]{1,0:T(8,128)}, f32[512,64]{1,0:T(8,128)S(1)}, u32[]{:S(2)}, u32[]{:S(2)}) collective-permute-start(f32[512,64]{1,0:T(8,128)} %squeeze.53), channel_id=1, source_target_pairs={{1,0},{2,1},{3,2},{4,3},{5,4},{6,5},{7,6},{8,7},{9,8},{10,9},{11,1... | collective-permute-start | bytes 393224 | tf_op jit(solution)/shard_map/ppermute | solution.py:13
Sparse Core Ops, SparseCore 0:
  28.6 70.0 all-gather.2
  119.9 66.9 all-gather.4
